TPU v7x, 32 devices: a whole 2x2x4 slice. The times are simulated.
32 devices in a mesh: row: 4 (over x, core), col: 8 (over z, y).
Axes of the slice: x: 2, y: 2, z: 4, core: 2. Of those that a mesh axis runs over, the one named last changes fastest.
Arguments:
- users: bfloat16 [32768, 256], P(('row', 'col')), may hold values from -20 to 20
- positives: int32 [32768], P(('row', 'col')), may hold values from 0 to 511
- items: bfloat16 [512, 256], P(('row', 'col')), may hold values from -6 to 6
- item_ids: int32 [512], P(('row', 'col')), may hold values from 0 to 999999
Outputs:
- loss: float32 [32768], P(('row', 'col'))
All inputs are finite; a program needn't handle non-finite values.
Results may differ from a plain program's by a relative error of at most 0.0003.
Values may be sent and summed in bfloat16 or wider, within the bound.
A program may use at most 128 MiB of HBM per device.

v0:
```python
import jax
import jax.numpy as jnp
from jax import lax
from jax.sharding import PartitionSpec as P


def absorb(carry, users, positives, pos_id, table, piece, where_at):
    high, summed, chosen = carry
    scores = 0.125 * lax.dot_general(
        users, piece, (((1,), (1,)), ((), ())), preferred_element_type=jnp.float32
    )
    ids = jnp.take(table, where_at)
    hit = where_at[None, :] == positives[:, None]
    keep = (ids[None, :] != pos_id[:, None]) | hit
    masked = jnp.where(keep, scores, -1e30)
    new_high = jnp.maximum(high, jnp.max(masked, axis=1))
    terms = jnp.where(keep, jnp.exp(masked - new_high[:, None]), 0.0)
    summed = jnp.sum(terms, axis=1)
    chosen = jnp.sum(jnp.where(hit, scores, 0.0), axis=1)
    return (new_high, summed, chosen)


def per_device(users, positives, items, item_ids):
    table = lax.all_gather(item_ids, ("row", "col"), axis=0, tiled=True)
    pos_id = jnp.take(table, positives)
    user_rows = users.shape[0]
    init = (
        jnp.full((user_rows,), -1e30, jnp.float32),
        jnp.zeros((user_rows,), jnp.float32),
        jnp.zeros((user_rows,), jnp.float32),
    )
    piece = lax.all_gather(items, ("row", "col"), axis=0, tiled=True)
    where_at = jnp.arange(piece.shape[0], dtype=jnp.int32)
    carry = absorb(init, users, positives, pos_id, table, piece, where_at)
    high, summed, chosen = carry
    return high + jnp.log(summed) - chosen


def solution(mesh):
    in_specs = (
        P(("row", "col"), None),
        P(("row", "col")),
        P(("row", "col"), None),
        P(("row", "col")),
    )
    out_specs = P(("row", "col"))
    return jax.shard_map(
        per_device, mesh=mesh, in_specs=in_specs, out_specs=out_specs, check_vma=False
    )
```

profile of v0, /device:TPU:0, one launch (start us, length us, event | category | flops | bytes accessed | tf_op | source)
XLA Modules:
  0.0 123.0 jit_solution(11870605535669868126)
XLA Ops:
  0.0 0.0 copy-start
  0.0 0.0 copy-start.1
  0.0 0.9 dynamic-update-slice
  0.9 42.0 %all-reduce = s32[512]{0:T(512)S(1)} all-reduce(s32[512]{0:T(512)S(1)} %dynamic-update-slice), channel_id=1, replica_groups=mesh['row'=4,'col'=8] {'row','col'}, use_global_device_ids=true, to_apply=%add | all-reduce | flops 512 | bytes 4096
  42.9 3.5 %gather_fusion = s32[512]{0:T(512)S(1)} fusion(s32[512]{0:T(512)S(1)} %all-reduce, s32[1024]{0:T(1024)S(1)} %pad_clamp_fusion), kind=kCustom, calls=%fused_computation | custom fusion | bytes 6144 | tf_op jit(solution)/shard_map/jit(_take)/gather | solution.py:12
  46.4 0.0 copy-done.1
  46.4 0.0 copy-start.2
  46.4 6.9 %gather_fusion.1 = s32[1024]{0:T(1024)S(1)} fusion(s32[512]{0:T(512)S(1)} %all-reduce, s32[1024]{0:T(1024)S(1)} %fusion.2), kind=kCustom, calls=%fused_computation.1 | custom fusion | bytes 12288 | tf_op jit(solution)/shard_map/jit(_take)/gather | solution.py:25
  53.3 0.0 copy-done.2
  53.3 67.4 %all_gather.7 = bf16[512,256]{1,0:T(8,128)(2,1)S(1)} all-gather(bf16[16,256]{1,0:T(8,128)(2,1)S(1)} %copy-done.2), channel_id=1, replica_groups=mesh['row'=4,'col'=8] {'row','col'}, dimensions={0}, use_global_device_ids=true | all-gather | bytes 270336 | tf_op jit(solution)/shard_map/all_gather | solution.py:32
  120.7 0.0 copy-done
  120.7 0.6 fusion.1
  121.4 1.0 select_reduce_fusion.1
  122.4 0.6 add_subtract_fusion
  (7 shorter events, 0.0 us)
Async XLA Ops:
  0.0 120.7 %copy-start = (bf16[1024,256]{1,0:T(8,128)(2,1)S(1)}, bf16[1024,256]{1,0:T(8,128)(2,1)}, u32[]{:S(2)}) copy-start(bf16[1024,256]{1,0:T(8,128)(2,1)} %param.4) | copy-start | bytes 1572868
  0.0 46.4 %copy-start.1 = (s32[1024]{0:T(1024)S(1)}, s32[1024]{0:T(1024)}, u32[]{:S(2)}) copy-start(s32[1024]{0:T(1024)} %param.5) | copy-start | bytes 12292
  46.4 6.9 %copy-start.2 = (bf16[16,256]{1,0:T(8,128)(2,1)S(1)}, bf16[16,256]{1,0:T(8,128)(2,1)}, u32[]{:S(2)}) copy-start(bf16[16,256]{1,0:T(8,128)(2,1)} %param.6) | copy-start | bytes 24580
where the time goes:
time: 123 us
  blocking collectives  109 us (89%)
  local copies, waits for them, and re-layouts  11.3 us (9%)
  other arithmetic  1.67 us (1%)
    all_gather x1, blocking collectives, per_device(): piece = lax.all_gather(items, ('row', 'col'), axis=0, tiled=True)  67.4 us
    unnamed x1, blocking collectives  42 us
    gather x1, local copies, waits for them, and re-layouts, per_device(): pos_id = jnp.take(table, positives)  6.87 us
    gather x1, local copies, waits for them, and re-layouts, absorb(): ids = jnp.take(table, where_at)  3.49 us

commit v1 on v0

v1 whole, which is shorter than its diff:
```python
import functools
import math

import jax
import jax.numpy as jnp
from jax import lax
from jax.experimental import pallas as pl
from jax.experimental.pallas import tpu as pltpu
from jax.sharding import PartitionSpec as P

MESH = pl.DeviceIdType.MESH
TWO_LEVEL = False
LOG2E = math.log2(math.e)
LOW = -1e30


def div(a, b):
    return a // b if isinstance(a, int) else lax.div(a, jnp.int32(b))


def rem(a, b):
    return a % b if isinstance(a, int) else lax.rem(a, jnp.int32(b))


def flip(z, k, n):
    if n & (n - 1):
        return rem(z + k, n)
    out, bit = 0, 1
    while bit < n:
        out = out + bit * rem(rem(div(z, bit), 2) + rem(div(k, bit), 2), 2)
        bit *= 2
    return out


def loop(n, body, limit=64):
    if n <= limit:
        for i in range(n):
            body(i)
    else:
        lax.fori_loop(0, n, lambda i, c: (body(i), c)[1], 0)


def kernel(nrow, ncol, users_hbm, pos_hbm, items_hbm, ids_hbm, out_ref,
           users, pos, pool, ids, tab, state, local_sem, send_sem, recv_sem,
           id_send, id_recv):
    ny = 2 if ncol % 2 == 0 else 1
    nz = ncol // ny
    group = nrow * ny
    count = nrow * ncol
    depth = pool.shape[1]
    chunks = users.shape[0] // 128
    rows = group * depth
    row, col = lax.axis_index("row"), lax.axis_index("col")
    z, y = div(col, ny), rem(col, ny)

    def slot_of(r, zi, yi):
        return zi * group + r * ny + yi

    mine = slot_of(row, z, y)

    def peer(k):
        kz, q = div(k, group), rem(k, group)
        r = rem(row + div(q, ny), nrow)
        yi = rem(y + rem(q, ny), ny)
        zi = flip(z, kz, nz)
        return r, zi * ny + yi, slot_of(r, zi, yi)

    own = pltpu.make_async_copy(items_hbm, pool.at[mine], local_sem.at[0])
    own_ids = pltpu.make_async_copy(ids_hbm, ids.at[mine], local_sem.at[1])
    own_users = pltpu.make_async_copy(users_hbm, users, local_sem.at[2])
    own_pos = pltpu.make_async_copy(pos_hbm, pos, local_sem.at[3])
    own_ids.start()
    own.start()
    own_pos.start()
    own_users.start()

    barrier = pltpu.get_barrier_semaphore()

    def greet(i):
        r, c, _ = peer(i + 1)
        pl.semaphore_signal(barrier, inc=1, device_id=(r, c), device_id_type=MESH)

    loop(count - 1, greet)
    own_ids.wait()
    own.wait()
    pl.semaphore_wait(barrier, count - 1)

    def id_copy(k):
        r, c, s = peer(k)
        return pltpu.make_async_remote_copy(
            src_ref=ids.at[mine], dst_ref=ids.at[mine], send_sem=id_send.at[s],
            recv_sem=id_recv.at[mine], device_id=(r, c), device_id_type=MESH)

    def item_copy(k):
        r, c, s = peer(k)
        return pltpu.make_async_remote_copy(
            src_ref=pool.at[mine], dst_ref=pool.at[mine], send_sem=send_sem.at[s],
            recv_sem=recv_sem.at[mine], device_id=(r, c), device_id_type=MESH)

    def arrival(buf, sems, s):
        return pltpu.make_async_copy(buf.at[s], buf.at[s], sems.at[s])

    loop(count - 1, lambda i: id_copy(count - 1 - i).start())
    loop(count - 1, lambda i: item_copy(count - 1 - i).start())

    own_pos.wait()
    p = pos[...]
    d, lane = p // depth, p % depth
    r, c = d // ncol, d % ncol
    slot = (c // ny) * group + r * ny + c % ny
    place = slot * depth + lane

    state[0] = jnp.full(state.shape[1:], LOW, jnp.float32)
    state[1] = jnp.zeros(state.shape[1:], jnp.float32)
    state[2] = jnp.zeros(state.shape[1:], jnp.float32)

    def wait_ids(i):
        _, _, s = peer(i + 1)
        arrival(ids, id_recv, s).wait()

    loop(count - 1, wait_ids)
    flat = ids[...].reshape(count, depth)
    tab[...] = jnp.concatenate(
        [flat, jnp.zeros((count, 128 - depth), jnp.int32)], axis=1)

    def look(t, found):
        line = jnp.broadcast_to(tab[pl.ds(t, 1), :], p.shape)
        got = jnp.take_along_axis(line, lane, axis=1, mode="promise_in_bounds")
        return jnp.where(slot == t, got, found)

    pid = jnp.zeros(p.shape, jnp.int32)
    if count <= 64:
        for t in range(count):
            pid = look(t, pid)
    else:
        pid = lax.fori_loop(0, count, look, pid)
    pid = pid.astype(jnp.float32)

    own_users.wait()
    eye = (lax.broadcasted_iota(jnp.int32, (1, depth, depth), 1)
           == lax.broadcasted_iota(jnp.int32, (1, depth, depth), 2))

    def absorb(kz):
        zi = flip(z, kz, nz)

        def wait_items(q):
            _, _, s = peer(kz * group + q)
            if isinstance(kz, int) and isinstance(q, int):
                if kz == 0 and q == 0:
                    return
                arrival(pool, recv_sem, s).wait()
            else:
                @pl.when(kz * group + q > 0)
                def _():
                    arrival(pool, recv_sem, s).wait()

        loop(group, wait_items)
        block = pool[pl.ds(zi * group, group)].reshape(rows, pool.shape[2])
        names = ids[pl.ds(zi * group, group)].astype(jnp.float32)
        names = jnp.broadcast_to(names, (group, depth, depth))
        names = jnp.sum(jnp.where(eye, names, 0.0), axis=2, keepdims=True)
        names = jnp.broadcast_to(names.reshape(rows, 1), (rows, 128))
        at = lax.broadcasted_iota(jnp.int32, (rows, 128), 0)
        here = place - zi * rows
        for i in range(chunks):
            x = lax.dot_general(
                block, users[pl.ds(i * 128, 128), :], (((1,), (1,)), ((), ())),
                preferred_element_type=jnp.float32) * (0.125 * LOG2E)
            hit = at == here[i:i + 1, :]
            keep = (names != pid[i:i + 1, :]) | hit
            masked = jnp.where(keep, x, LOW).reshape(rows // 8, 8, 128)
            high = state[0, i]
            top = jnp.maximum(high, jnp.max(masked, axis=0))
            terms = jnp.sum(jnp.exp2(masked - top[None]), axis=0)
            state[1, i] = state[1, i] * jnp.exp2(high - top) + terms
            state[0, i] = top
            state[2, i] = state[2, i] + jnp.sum(
                jnp.where(hit, x, 0.0).reshape(rows // 8, 8, 128), axis=0)

    loop(nz, absorb, 4)

    for i in range(chunks):
        high = state[0, i]
        top = jnp.max(high, axis=0, keepdims=True)
        total = jnp.sum(state[1, i] * jnp.exp2(high - top), axis=0, keepdims=True)
        chosen = jnp.sum(state[2, i], axis=0, keepdims=True)
        out_ref[i:i + 1, :] = (top - chosen) * (1.0 / LOG2E) + jnp.log(total)

    def finish(i):
        id_copy(i + 1).wait_send()
        item_copy(i + 1).wait_send()

    loop(count - 1, finish)


def solution(mesh):
    nrow, ncol = mesh.shape["row"], mesh.shape["col"]
    count = nrow * ncol

    def per_device(users, positives, items, item_ids):
        n, width = users.shape
        depth = items.shape[0]
        lines = n // 128
        out = pl.pallas_call(
            functools.partial(kernel, nrow, ncol),
            out_shape=jax.ShapeDtypeStruct((lines, 128), jnp.float32),
            in_specs=[pl.BlockSpec(memory_space=pl.ANY)] * 4,
            out_specs=pl.BlockSpec(memory_space=pltpu.VMEM),
            scratch_shapes=[
                pltpu.VMEM((n, width), users.dtype),
                pltpu.VMEM((lines, 128), jnp.int32),
                pltpu.VMEM((count, depth, width), items.dtype),
                pltpu.VMEM((count, 1, depth), jnp.int32),
                pltpu.VMEM((count, 128), jnp.int32),
                pltpu.VMEM((3, lines, 8, 128), jnp.float32),
                pltpu.SemaphoreType.DMA((4,)),
                pltpu.SemaphoreType.DMA((count,)),
                pltpu.SemaphoreType.DMA((count,)),
                pltpu.SemaphoreType.DMA((count,)),
                pltpu.SemaphoreType.DMA((count,)),
            ],
            compiler_params=pltpu.CompilerParams(
                collective_id=0, has_side_effects=True),
        )(users, positives.reshape(lines, 128), items, item_ids.reshape(1, depth))
        return out.reshape(n)

    in_specs = (
        P(("row", "col"), None),
        P(("row", "col")),
        P(("row", "col"), None),
        P(("row", "col")),
    )
    return jax.shard_map(
        per_device, mesh=mesh, in_specs=in_specs, out_specs=P(("row", "col")),
        check_vma=False)
```

time: 123 us -> 18.6 us (0.15)
  blocking collectives: 109 us -> 0 us
  Pallas kernels: 0 us -> 17.2 us
  local copies, waits for them, and re-layouts: 11.3 us -> 1.28 us
  other arithmetic: 1.67 us -> 0 us
    all_gather x1 -> x0, blocking collectives: 67.4 us -> none  [per_device(): piece = lax.all_gather(items, ('row', 'col'), axis=0, tiled=True)]
    unnamed x1 -> x0, blocking collectives: 42 us -> none
    pallas_call x0 -> x1, Pallas kernels: none -> 17.2 us  [per_device(): pl.pallas_call(functools.partial(kernel, nrow, ncol), out_shape=jax.Shape...]
    gather x2 -> x0, local copies, waits for them, and re-layouts: 10.4 us -> none  [the longest x1 6.87 us: per_device(): pos_id = jnp.take(table, positives)]
where the time goes in v1:
time: 18.6 us; the launch traced here: 18.4 us
  Pallas kernels  17.2 us (92%)
  local copies, waits for them, and re-layouts  1.28 us (7%)
    pallas_call x1, Pallas kernels, per_device(): pl.pallas_call(functools.partial(kernel, nrow, ncol), out_shape=jax.Shape...  17.2 us
    unnamed x1, local copies, waits for them, and re-layouts  1.28 us

profile of v1, /device:TPU:0, one launch (start us, length us, event | category | flops | bytes accessed | tf_op | source)
XLA Modules:
  0.0 18.4 jit_solution(10275309836827308185)
XLA Ops:
  0.0 17.2 %shard_map.46 = f32[8,128]{1,0:T(8,128)} custom-call(bf16[1024,256]{1,0:T(8,128)(2,1)} %users_hbm.1, s32[8,128]{1,0:T(8,128)} %bitcast.4, bf16[16,256]{1,0:T(8,128)(2,1)} %items_hbm.1, s32[1,16]{1,0:T(1,128)} %bitcast.5), custom_call_target="tpu_custom_call" | custom-call | tf_op jit(solution)/shard_map/pallas_call | solution.py:204
  17.2 1.3 %copy.6 = f32[1024]{0:T(1024)} copy(f32[1024]{0:T(1024)} %bitcast.3) | data formatting | bytes 8192

commit v2 on v1

--- a/solution.py
+++ b/solution.py
@@ -9,7 +9,6 @@
 from jax.sharding import PartitionSpec as P
 
 MESH = pl.DeviceIdType.MESH
-TWO_LEVEL = False
 LOG2E = math.log2(math.e)
 LOW = -1e30
 
@@ -58,12 +57,20 @@
 
     mine = slot_of(row, z, y)
 
-    def peer(k):
-        kz, q = div(k, group), rem(k, group)
-        r = rem(row + div(q, ny), nrow)
+    core = rem(row, 2)
+    fan = nrow // 2 * ny
+    chips = nz * fan
+    mate = (row + 1 - 2 * core, col)
+
+    def chip(k):
+        kz, q = div(k, fan), rem(k, fan)
+        r = rem(div(row, 2) + div(q, ny), nrow // 2) * 2 + core
         yi = rem(y + rem(q, ny), ny)
         zi = flip(z, kz, nz)
         return r, zi * ny + yi, slot_of(r, zi, yi)
+
+    def mate_slot(k):
+        return chip(k)[2] + (1 - 2 * core) * ny
 
     own = pltpu.make_async_copy(items_hbm, pool.at[mine], local_sem.at[0])
     own_ids = pltpu.make_async_copy(ids_hbm, ids.at[mine], local_sem.at[1])
@@ -77,31 +84,41 @@
     barrier = pltpu.get_barrier_semaphore()
 
     def greet(i):
-        r, c, _ = peer(i + 1)
+        r, c, _ = chip(chips - 1 - i)
         pl.semaphore_signal(barrier, inc=1, device_id=(r, c), device_id_type=MESH)
 
-    loop(count - 1, greet)
+    loop(chips - 1, greet)
+    pl.semaphore_signal(barrier, inc=1, device_id=mate, device_id_type=MESH)
     own_ids.wait()
     own.wait()
-    pl.semaphore_wait(barrier, count - 1)
-
-    def id_copy(k):
-        r, c, s = peer(k)
+    pl.semaphore_wait(barrier, chips)
+
+    def push(buf, sends, recvs, s, n, r, c):
         return pltpu.make_async_remote_copy(
-            src_ref=ids.at[mine], dst_ref=ids.at[mine], send_sem=id_send.at[s],
-            recv_sem=id_recv.at[mine], device_id=(r, c), device_id_type=MESH)
-
-    def item_copy(k):
-        r, c, s = peer(k)
-        return pltpu.make_async_remote_copy(
-            src_ref=pool.at[mine], dst_ref=pool.at[mine], send_sem=send_sem.at[s],
-            recv_sem=recv_sem.at[mine], device_id=(r, c), device_id_type=MESH)
+            src_ref=buf.at[s], dst_ref=buf.at[s], send_sem=sends.at[n],
+            recv_sem=recvs.at[s], device_id=(r, c), device_id_type=MESH)
+
+    def id_out(k):
+        r, c, _ = chip(k)
+        return push(ids, id_send, id_recv, mine, k, r, c)
+
+    def item_out(k):
+        r, c, _ = chip(k)
+        return push(pool, send_sem, recv_sem, mine, k, r, c)
+
+    def id_over(k):
+        return push(ids, id_send, id_recv, chip(k)[2], chips + k, *mate)
+
+    def item_over(k):
+        return push(pool, send_sem, recv_sem, chip(k)[2], chips + k, *mate)
 
     def arrival(buf, sems, s):
         return pltpu.make_async_copy(buf.at[s], buf.at[s], sems.at[s])
 
-    loop(count - 1, lambda i: id_copy(count - 1 - i).start())
-    loop(count - 1, lambda i: item_copy(count - 1 - i).start())
+    loop(chips - 1, lambda i: id_out(chips - 1 - i).start())
+    loop(chips - 1, lambda i: item_out(chips - 1 - i).start())
+    id_over(0).start()
+    item_over(0).start()
 
     own_pos.wait()
     p = pos[...]
@@ -114,11 +131,18 @@
     state[1] = jnp.zeros(state.shape[1:], jnp.float32)
     state[2] = jnp.zeros(state.shape[1:], jnp.float32)
 
-    def wait_ids(i):
-        _, _, s = peer(i + 1)
-        arrival(ids, id_recv, s).wait()
-
-    loop(count - 1, wait_ids)
+    def relay_ids(i):
+        arrival(ids, id_recv, chip(i + 1)[2]).wait()
+        id_over(i + 1).start()
+
+    def relay_items(i):
+        arrival(pool, recv_sem, chip(i + 1)[2]).wait()
+        item_over(i + 1).start()
+
+    loop(chips - 1, relay_ids)
+    early = (nz - 1) * fan - 1
+    loop(early, relay_items)
+    loop(chips, lambda k: arrival(ids, id_recv, mate_slot(k)).wait())
     flat = ids[...].reshape(count, depth)
     tab[...] = jnp.concatenate(
         [flat, jnp.zeros((count, 128 - depth), jnp.int32)], axis=1)
@@ -143,18 +167,8 @@
     def absorb(kz):
         zi = flip(z, kz, nz)
 
-        def wait_items(q):
-            _, _, s = peer(kz * group + q)
-            if isinstance(kz, int) and isinstance(q, int):
-                if kz == 0 and q == 0:
-                    return
-                arrival(pool, recv_sem, s).wait()
-            else:
-                @pl.when(kz * group + q > 0)
-                def _():
-                    arrival(pool, recv_sem, s).wait()
-
-        loop(group, wait_items)
+        loop(fan, lambda q: arrival(
+            pool, recv_sem, mate_slot(kz * fan + q)).wait())
         block = pool[pl.ds(zi * group, group)].reshape(rows, pool.shape[2])
         names = ids[pl.ds(zi * group, group)].astype(jnp.float32)
         names = jnp.broadcast_to(names, (group, depth, depth))
@@ -177,7 +191,13 @@
             state[2, i] = state[2, i] + jnp.sum(
                 jnp.where(hit, x, 0.0).reshape(rows // 8, 8, 128), axis=0)
 
-    loop(nz, absorb, 4)
+    absorb(0)
+    loop(fan, lambda q: relay_items(early + q))
+    if nz <= 4:
+        for kz in range(1, nz):
+            absorb(kz)
+    else:
+        lax.fori_loop(1, nz, lambda kz, c: (absorb(kz), c)[1], 0)
 
     for i in range(chunks):
         high = state[0, i]
@@ -187,10 +207,15 @@
         out_ref[i:i + 1, :] = (top - chosen) * (1.0 / LOG2E) + jnp.log(total)
 
     def finish(i):
-        id_copy(i + 1).wait_send()
-        item_copy(i + 1).wait_send()
-
-    loop(count - 1, finish)
+        id_out(i + 1).wait_send()
+        item_out(i + 1).wait_send()
+
+    def finish_over(k):
+        id_over(k).wait_send()
+        item_over(k).wait_send()
+
+    loop(chips - 1, finish)
+    loop(chips, finish_over)
 
 
 def solution(mesh):
@@ -203,7 +228,7 @@
         lines = n // 128
         out = pl.pallas_call(
             functools.partial(kernel, nrow, ncol),
-            out_shape=jax.ShapeDtypeStruct((lines, 128), jnp.float32),
+            out_shape=pltpu.VMEM((lines, 128), jnp.float32),
             in_specs=[pl.BlockSpec(memory_space=pl.ANY)] * 4,
             out_specs=pl.BlockSpec(memory_space=pltpu.VMEM),
             scratch_shapes=[

time: 18.6 us -> 14.7 us (0.79)
  Pallas kernels: 17.2 us -> 14 us
  local copies, waits for them, and re-layouts: 1.28 us -> 0.6 us
    pallas_call x1, Pallas kernels: 17.2 us -> 14 us  [per_device(): pl.pallas_call(functools.partial(kernel, nrow, ncol), out_shape=pltpu.VME...]
    unnamed x1, local copies, waits for them, and re-layouts: 1.28 us -> 0.6 us
where the time goes in v2:
time: 14.7 us; the launch traced here: 14.6 us
  Pallas kernels  14 us (95%)
  local copies, waits for them, and re-layouts  0.6 us (4%)
    pallas_call x1, Pallas kernels, per_device(): pl.pallas_call(functools.partial(kernel, nrow, ncol), out_shape=pltpu.VME...  14 us
    unnamed x1, local copies, waits for them, and re-layouts  0.6 us

profile of v2, /device:TPU:0, one launch (start us, length us, event | category | flops | bytes accessed | tf_op | source)
XLA Modules:
  0.0 14.6 jit_solution(17741482800826695571)
XLA Ops:
  0.0 14.0 %shard_map.46 = f32[8,128]{1,0:T(8,128)S(1)} custom-call(bf16[1024,256]{1,0:T(8,128)(2,1)} %users_hbm.1, s32[8,128]{1,0:T(8,128)} %bitcast.4, bf16[16,256]{1,0:T(8,128)(2,1)} %items_hbm.1, s32[1,16]{1,0:T(1,128)} %bitcast.5), custom_call_target="tpu_custom_call" | custom-call | tf_op jit(solution)/shard_map/pallas_call | solution.py:229
  14.0 0.6 %copy.6 = f32[1024]{0:T(1024)} copy(f32[1024]{0:T(1024)S(1)} %bitcast.3) | data formatting | bytes 8192
